TPU v7x, 32 devices: a whole 2x2x4 slice. The times are simulated.
32 devices in a mesh: groups: 2 (over y), dp: 2 (over core), tensor: 8 (over z, x).
Axes of the slice: x: 2, y: 2, z: 4, core: 2. Of those that a mesh axis runs over, the one named last changes fastest.
Arguments:
- hidden_in: bfloat16 [4, 1024, 5120], P(('groups', 'dp'), 'tensor'), parts along dimension 0, may hold values from -40 to 40
- first_values: bfloat16 [4, 1024, 1024], P(('groups', 'dp'), 'tensor'), parts along dimension 0, may hold values from -6 to 6
- qkv_weight: bfloat16 [5120, 3, 1024], P(None, None, 'tensor'), may hold values from -1 to 1
- out_weight: bfloat16 [1024, 5120], P('tensor'), may hold values from -0.1875 to 0.1875
- mix_table: float32 [8, 2], replicated, may hold values from 0.2 to 1
- mix_index: int32 [8], P('tensor'), may hold values from 0 to 7
- lengths: int32 [4], P(('groups', 'dp')), parts along dimension 0, may hold values from 256 to 1024
Outputs:
- attn_out: bfloat16 [4, 1024, 5120], P(('groups', 'dp'), 'tensor'), parts along dimension 0
There are 2 independent parts, one for each index of `groups`. A program takes and returns all parts, laid end to end along the dimension named above; an argument that names none is the same for every part. Nothing has to cross between parts.
All inputs are finite; a program needn't handle non-finite values.
Results may differ from a plain program's by a relative error of at most 0.0077.
Values may be sent and summed in bfloat16 or wider, within the bound.
A program may use at most 128 MiB of HBM per device.

v0:
```python
import math

import jax
import jax.numpy as jnp
from jax import lax
from jax.sharding import PartitionSpec as P

NEG_FILL = -1e30


def body(hidden_in, first_values, qkv_weight, out_weight, mix_table, mix_index, lengths):
    local_rows = hidden_in[0]
    model_width = local_rows.shape[1]
    head_width = qkv_weight.shape[2]
    heads_here = mix_index.shape[0]
    head_size = head_width // heads_here
    merged_weight = qkv_weight.reshape(model_width, 3 * head_width)
    projected = jnp.dot(
        lax.all_gather(local_rows, "tensor", axis=0, tiled=True),
        merged_weight,
        preferred_element_type=jnp.float32,
    ).astype(jnp.bfloat16)
    relaid = lax.all_to_all(first_values[0], "tensor", split_axis=1, concat_axis=0, tiled=True)
    total_rows = projected.shape[0]
    split_parts = projected.reshape(total_rows, 3, heads_here, head_size)
    queries = split_parts[:, 0]
    key_rows = split_parts[:, 1]
    firsts = relaid.reshape(total_rows, heads_here, head_size)
    levels = mix_table.shape[0]
    one_hot = (mix_index[:, None] == jnp.arange(levels, dtype=jnp.int32)[None, :]).astype(
        jnp.float32
    )
    weights_mix = jnp.dot(one_hot, mix_table, precision=lax.Precision.HIGHEST)
    mixed_values = (
        weights_mix[None, :, 0:1] * split_parts[:, 2].astype(jnp.float32)
        + weights_mix[None, :, 1:2] * firsts.astype(jnp.float32)
    ).astype(jnp.bfloat16)
    positions = jnp.arange(total_rows, dtype=jnp.int32)
    valid_length = lengths[0]
    score_scale = 1.0 / math.sqrt(head_size)
    block_rows = min(512, total_rows)

    def attend(first_row):
        query_block = lax.dynamic_slice_in_dim(queries, first_row, block_rows, 0)
        row_positions = first_row + jnp.arange(block_rows, dtype=jnp.int32)
        scores = (
            jnp.einsum("qhd,khd->hqk", query_block, key_rows, preferred_element_type=jnp.float32)
            * score_scale
        )
        allowed = (positions[None, :] <= row_positions[:, None]) & (
            positions[None, :] < valid_length
        )
        scores = jnp.where(allowed[None], scores, NEG_FILL)
        row_max = jnp.max(scores, axis=2, keepdims=True)
        raised = jnp.exp(scores - row_max)
        weights = (raised / jnp.sum(raised, axis=2, keepdims=True)).astype(jnp.bfloat16)
        return jnp.einsum(
            "hqk,khd->qhd", weights, mixed_values, preferred_element_type=jnp.float32
        ).astype(jnp.bfloat16)

    starts = jnp.arange(total_rows // block_rows, dtype=jnp.int32) * block_rows
    outputs = lax.map(attend, starts).reshape(total_rows, head_width)
    kept_rows = lax.psum_scatter(
        jnp.dot(outputs, out_weight, preferred_element_type=jnp.float32),
        "tensor",
        scatter_dimension=0,
        tiled=True,
    )
    return kept_rows.astype(jnp.bfloat16)[None]


def solution(mesh):
    placed = (
        P(("groups", "dp"), "tensor", None),
        P(("groups", "dp"), "tensor", None),
        P(None, None, "tensor"),
        P("tensor", None),
        P(),
        P("tensor"),
        P(("groups", "dp")),
    )
    return jax.shard_map(
        body,
        mesh=mesh,
        in_specs=placed,
        out_specs=P(("groups", "dp"), "tensor", None),
        check_vma=False,
    )
```

profile of v0, /device:TPU:0, one launch (start us, length us, event | category | flops | bytes accessed | tf_op | source)
XLA Modules:
  0.0 544.5 jit_solution(15887755591005693651)
XLA Ops:
  6.5 0.7 all-gather.3.cloned.1.call-update
  7.3 1.0 copy.20
  8.3 0.7 copy.16
  9.0 7.3 %all-to-all-start = ((bf16[128,8,128]{2,0,1:T(8,128)(2,1)}), bf16[128,8,128]{2,0,1:T(8,128)(2,1)S(1)}, u32[]{:S(2)}, u32[]{:S(2)}) async-start(bf16[128,8,128]{2,0,1:T(8,128)(2,1)} %copy.16), calls=%async_computation | async-start | bytes 524288 | tf_op jit(solution)/shard_map/all_to_all | solution.py:23
  17.0 6.4 %copy.12 = bf16[5120,3,128]{0,2,1:T(8,128)(2,1)} copy(bf16[5120,3,128]{2,0,1:T(8,128)(2,1)} %param.11) | data formatting | bytes 7864320 | tf_op args[2]
  23.4 0.1 fusion.17
  23.5 0.6 fusion.22
  24.2 1.2 all-to-all-done
  25.3 0.7 convert_multiply_fusion
  26.0 136.8 %all-gather.3.cloned.1.call-done = bf16[1,1024,5120]{2,1,0:T(8,128)(2,1)} async-done(((bf16[1,128,5120]{2,1,0:T(8,128)(2,1)}), bf16[1,1024,5120]{2,1,0:T(8,128)(2,1)}) %all-gather.3.cloned.1.call-update) | async-done | bytes 10485776 | tf_op jit(solution)/shard_map/all_gather | solution.py:19
  162.8 9.3 %fusion.13 = bf16[1024,384]{0,1:T(8,128)(2,1)S(1)} fusion(bf16[5120,384]{0,1:T(8,128)(2,1)} %bitcast.71, bf16[1,1024,5120]{2,1,0:T(8,128)(2,1)} %all-gather.3.cloned.1.call-done), kind=kOutput, calls=%fused_computation.19 | convolution fusion | flops 4026925056 | bytes 15204352 | tf_op jit(solution)/shard_map/dot_general | solution.py:18
  172.2 0.1 fusion.21
  172.2 0.2 copy.19
  172.4 0.2 copy.18
  172.6 0.2 copy.17
  172.8 0.8 fusion.16
  173.5 11.5 %while.12 = (s32[]{:T(128)}, bf16[2,512,1,128]{3,1,2,0:T(8,128)(2,1)S(1)}, s32[2]{0:T(128)S(1)}, s32[]{:T(128)}, bf16[1024,1,128]{2,0,1:T(8,128)(2,1)S(1)}, /*in...) while((s32[]{:T(128)}, ...), condition=%wide.region_3.4_spmd.clone.clone, body=%wide.region_0.3_spmd.clone.clone.sunk | while | flops 273744384 | bytes 7094443 | solution.py:62
  173.5 0.6 dynamic_slice.20
  176.1 0.7 iota_compare_fusion.3
  176.7 0.7 iota_add_fusion.2
  177.4 0.8 fusion.33
  178.2 0.5 fusion.34
  178.7 0.6 fusion.35
  179.3 0.6 dynamic_slice.20
  181.8 0.7 iota_compare_fusion.3
  182.5 0.7 iota_add_fusion.2
  183.1 0.8 fusion.33
  183.9 0.5 fusion.34
  184.4 0.6 fusion.35
  185.0 8.6 %fusion.23 = f32[1024,5120]{1,0:T(8,128)} fusion(bf16[1024,128]{1,0:T(8,128)(2,1)S(1)} %bitcast.75, bf16[128,5120]{1,0:T(8,128)(2,1)S(1)} %copy-done), kind=kOutput, calls=%fused_computation.32 | convolution fusion | flops 1342177280 | bytes 22544384 | tf_op jit(solution)/shard_map/dot_general | solution.py:64
  193.6 341.1 %reduce-scatter.2.cloned.1.call-done = f32[128,5120]{1,0:T(8,128)} async-done(((f32[1024,5120]{1,0:T(8,128)}), f32[128,5120]{1,0:T(8,128)}) %reduce-scatter.2.cloned.1.call-update) | async-done | bytes 2621456 | tf_op jit(solution)/shard_map/reduce_scatter | solution.py:63
  534.7 3.0 convert_bitcast_fusion
  (9 shorter events, 0.1 us)
Async XLA Ops:
  6.5 178.5 %copy-start = (bf16[128,5120]{1,0:T(8,128)(2,1)S(1)}, bf16[128,5120]{1,0:T(8,128)(2,1)}, u32[]{:S(2)}) copy-start(bf16[128,5120]{1,0:T(8,128)(2,1)} %param.12) | copy-start | bytes 3932164
  6.5 156.3 %all-gather.3.cloned.1.call-start = ((), (), s32[]{:S(2)}) async-start(), calls=%async_computation.3 | async-start | bytes 11796480 | tf_op jit(solution)/shard_map/all_gather | solution.py:19
  9.0 16.3 %all-to-all-start = ((bf16[128,8,128]{2,0,1:T(8,128)(2,1)}), bf16[128,8,128]{2,0,1:T(8,128)(2,1)S(1)}, u32[]{:S(2)}, u32[]{:S(2)}) async-start(bf16[128,8,128]{2,0,1:T(8,128)(2,1)} %copy.16), calls=%async_computation | async-start | bytes 524288 | tf_op jit(solution)/shard_map/all_to_all | solution.py:23
  16.3 518.4 %reduce-scatter.2.cloned.1.call-start = ((), (), s32[]{:S(2)}) async-start(), calls=%async_computation.2 | async-start | bytes 23592960 | tf_op jit(solution)/shard_map/reduce_scatter | solution.py:63
  17.0 6.4 %copy-start.1 = (f32[8,2]{0,1:T(2,128)S(1)}, f32[8,2]{0,1:T(2,128)}, u32[]{:S(2)}) copy-start(f32[8,2]{0,1:T(2,128)} %param.13) | copy-start | bytes 196
Sparse Core Ops, SparseCore 0:
  9.5 153.2 all-gather.2
  193.8 340.9 reduce-scatter.1
where the time goes:
time: 545 us
  waiting for transfers between devices  480 us (88%)
  matrix products  20.8 us (4%)
  between operations  14.1 us (3%)
  local copies, waits for them, and re-layouts  10.5 us (2%)
  other arithmetic  8.02 us (1%)
  starting transfers between devices  7.32 us (1%)
    reduce_scatter x1, waiting for transfers between devices, body(): lax.psum_scatter(jnp.dot(outputs, out_weight, preferred_element_type=jnp....  341 us
    all_gather x1, waiting for transfers between devices, body(): lax.all_gather(local_rows, 'tensor', axis=0, tiled=True)  137 us
  transfers between devices with their start and end apart: 3, of which 3 were waited for; matrix products, arithmetic and copies ran while one was open for 2% of the time, Pallas kernels for 0%

commit v1 on v0

v1 whole, which is shorter than its diff:
```python
import math

import jax
import jax.numpy as jnp
from jax import lax
from jax.sharding import PartitionSpec as P

NEG_FILL = -1e30
PAIR = 2


def attention(queries, key_rows, mixed_values, valid_length, head_size):
    total_rows = queries.shape[0]
    positions = jnp.arange(total_rows, dtype=jnp.int32)
    score_scale = 1.0 / math.sqrt(head_size)
    block_rows = min(512, total_rows)
    outputs = []
    for first_row in range(0, total_rows, block_rows):
        stop = first_row + block_rows
        scores = (
            jnp.einsum(
                "qhd,khd->hqk",
                queries[first_row:stop],
                key_rows[:stop],
                preferred_element_type=jnp.float32,
            )
            * score_scale
        )
        keys_at, rows_at = positions[:stop], positions[first_row:stop]
        allowed = (keys_at[None, :] <= rows_at[:, None]) & (keys_at[None, :] < valid_length)
        scores = jnp.where(allowed[None], scores, NEG_FILL)
        row_max = jnp.max(scores, axis=2, keepdims=True)
        raised = jnp.exp(scores - row_max)
        weights = (raised / jnp.sum(raised, axis=2, keepdims=True)).astype(jnp.bfloat16)
        outputs.append(
            jnp.einsum(
                "hqk,khd->qhd", weights, mixed_values[:stop], preferred_element_type=jnp.float32
            ).astype(jnp.bfloat16)
        )
    return jnp.concatenate(outputs, axis=0)


def body(hidden_in, first_values, qkv_weight, out_weight, mix_table, mix_index, lengths):
    local_rows = hidden_in[0]
    own_rows, model_width = local_rows.shape
    head_width = qkv_weight.shape[2]
    heads_here = mix_index.shape[0]
    head_size = head_width // heads_here
    ranks = lax.axis_size("tensor")
    cores = lax.axis_size("dp")
    rank = lax.axis_index("tensor")
    core = lax.axis_index("dp")
    side = rank % PAIR
    line = ranks // PAIR
    swap_pair = [(r, r ^ 1) for r in range(ranks)]
    swap_core = [(c, c ^ 1) for c in range(cores)]

    own_w = qkv_weight.reshape(model_width, 3 * head_width)
    half = model_width // 2
    sent = lax.dynamic_slice_in_dim(own_w, core * half, half, 0)
    got = lax.ppermute(sent, "tensor", swap_pair)
    got_other = lax.ppermute(got, "dp", swap_core)
    pair_w = jnp.where(
        core == 0,
        jnp.concatenate([got, got_other], axis=0),
        jnp.concatenate([got_other, got], axis=0),
    )

    lines = [[s + PAIR * i for i in range(line)] for s in range(PAIR)]
    rows = lax.all_gather(local_rows, "tensor", axis=0, tiled=True, axis_index_groups=lines)
    for_pair = jnp.dot(rows, pair_w, preferred_element_type=jnp.float32).astype(jnp.bfloat16)
    from_pair = lax.ppermute(for_pair, "tensor", swap_pair)
    ours = jnp.dot(rows, own_w, preferred_element_type=jnp.float32).astype(jnp.bfloat16)
    ours = ours.reshape(line, own_rows, 3 * head_width)
    from_pair = from_pair.reshape(line, own_rows, 3 * head_width)
    projected = jnp.where(
        side == 0,
        jnp.stack([ours, from_pair], axis=1),
        jnp.stack([from_pair, ours], axis=1),
    )
    total_rows = ranks * own_rows
    split_parts = projected.reshape(total_rows, 3, heads_here, head_size)

    relaid = lax.all_to_all(first_values[0], "tensor", split_axis=1, concat_axis=0, tiled=True)
    firsts = relaid.reshape(total_rows, heads_here, head_size)
    levels = mix_table.shape[0]
    one_hot = (mix_index[:, None] == jnp.arange(levels, dtype=jnp.int32)[None, :]).astype(
        jnp.float32
    )
    weights_mix = jnp.dot(one_hot, mix_table, precision=lax.Precision.HIGHEST)
    mixed_values = (
        weights_mix[None, :, 0:1] * split_parts[:, 2].astype(jnp.float32)
        + weights_mix[None, :, 1:2] * firsts.astype(jnp.float32)
    ).astype(jnp.bfloat16)
    attended = attention(
        split_parts[:, 0], split_parts[:, 1], mixed_values, lengths[0], head_size
    ).reshape(total_rows, head_width)

    gathered_bytes = ranks * out_weight.size * 2
    summed_bytes = total_rows * model_width * 4
    if gathered_bytes > summed_bytes:
        kept_rows = lax.psum_scatter(
            jnp.dot(attended, out_weight, preferred_element_type=jnp.float32),
            "tensor",
            scatter_dimension=0,
            tiled=True,
        )
        return kept_rows.astype(jnp.bfloat16)[None]

    part = head_width // 2
    own_part = lax.dynamic_slice_in_dim(out_weight, core * part, part, 0)
    mine = lax.all_gather(own_part, "tensor", axis=0, tiled=True)
    other = lax.ppermute(mine, "dp", swap_core)
    kept = lax.all_to_all(attended, "tensor", split_axis=0, concat_axis=1, tiled=True)
    kept = kept.reshape(own_rows, ranks, 2, part)
    low = kept[:, :, 0].reshape(own_rows, ranks * part)
    high = kept[:, :, 1].reshape(own_rows, ranks * part)
    out = jnp.dot(
        jnp.where(core == 0, low, high), mine, preferred_element_type=jnp.float32
    ) + jnp.dot(jnp.where(core == 0, high, low), other, preferred_element_type=jnp.float32)
    return out.astype(jnp.bfloat16)[None]


def solution(mesh):
    placed = (
        P(("groups", "dp"), "tensor", None),
        P(("groups", "dp"), "tensor", None),
        P(None, None, "tensor"),
        P("tensor", None),
        P(),
        P("tensor"),
        P(("groups", "dp")),
    )
    return jax.shard_map(
        body,
        mesh=mesh,
        in_specs=placed,
        out_specs=P(("groups", "dp"), "tensor", None),
        check_vma=False,
    )
```

time: 545 us -> 275 us (0.50)
  waiting for transfers between devices: 480 us -> 193 us
  blocking collectives: 0 us -> 11.2 us
  local copies, waits for them, and re-layouts: 10.5 us -> 18.7 us
    reduce_scatter x1 -> x0, waiting for transfers between devices: 341 us -> none  [body(): lax.psum_scatter(jnp.dot(outputs, out_weight, preferred_element_type=jnp....]
    ppermute x0 -> x4, waiting for transfers between devices: none -> 72 us  [the longest x1 66 us: body(): got = lax.ppermute(sent, 'tensor', swap_pair)]
    all_gather x1 -> x2, waiting for transfers between devices: 137 us -> 121 us  [the longest x1 99 us: body(): lax.all_gather(local_rows, 'tensor', axis=0, tiled=True, axis_index_group...]
    all_to_all x0 -> x1, blocking collectives: none -> 11.2 us  [body(): lax.all_to_all(attended, 'tensor', split_axis=0, concat_axis=1, tiled=True)]
    dot_general x6 -> x8, matrix products: 20.7 us -> 18.7 us  [the longest x1 7.32 us: body(): jnp.dot(rows, pair_w, preferred_element_type=jnp.float32)]
  transfers between devices with their start and end apart: 3 -> 7, of which waited for: 3 -> 4; matrix products, arithmetic and copies ran while one was open for 2% -> 13% of each run, Pallas kernels for 0% -> 0%
where the time goes in v1:
time: 275 us
  waiting for transfers between devices  193 us (70%)
  matrix products  18.8 us (7%)
  local copies, waits for them, and re-layouts  18.7 us (7%)
  between operations  15 us (5%)
  starting transfers between devices  11.5 us (4%)
  blocking collectives  11.2 us (4%)
  other arithmetic  6.28 us (2%)
    all_gather x1, waiting for transfers between devices, body(): lax.all_gather(local_rows, 'tensor', axis=0, tiled=True, axis_index_group...  99 us
    ppermute x1, waiting for transfers between devices, body(): got = lax.ppermute(sent, 'tensor', swap_pair)  66 us
    all_gather x1, waiting for transfers between devices, body(): mine = lax.all_gather(own_part, 'tensor', axis=0, tiled=True)  21.7 us
    all_to_all x1, blocking collectives, body(): lax.all_to_all(attended, 'tensor', split_axis=0, concat_axis=1, tiled=True)  11.2 us
    unnamed x22, local copies, waits for them, and re-layouts  9.38 us
    dot_general x1, matrix products, body(): jnp.dot(rows, pair_w, preferred_element_type=jnp.float32)  7.32 us
    all_to_all x1, starting transfers between devices, body(): lax.all_to_all(first_values[0], 'tensor', split_axis=1, concat_axis=0, ti...  6.89 us
    ppermute x1, waiting for transfers between devices, body(): from_pair = lax.ppermute(for_pair, 'tensor', swap_pair)  5.95 us
  transfers between devices with their start and end apart: 7, of which 4 were waited for; matrix products, arithmetic and copies ran while one was open for 13% of the time, Pallas kernels for 0%

profile of v1, /device:TPU:0, one launch (start us, length us, event | category | flops | bytes accessed | tf_op | source)
XLA Modules:
  0.0 274.8 jit_solution(7623524188530878765)
XLA Ops:
  6.5 1.3 copy-done
  7.9 0.9 constant_dynamic-slice_fusion
  8.8 0.7 all-gather.6.cloned.1.call-update
  9.5 6.3 %copy.22 = bf16[5120,3,128]{0,2,1:T(8,128)(2,1)} copy(bf16[5120,3,128]{2,0,1:T(8,128)(2,1)} %param.9) | data formatting | bytes 7864320 | tf_op args[2]
  15.8 1.7 constant_dynamic-slice_fusion.1
  17.5 3.0 %collective-permute-start = (bf16[2560,384]{0,1:T(8,128)(2,1)S(1)}, bf16[2560,384]{0,1:T(8,128)(2,1)}, u32[]{:S(2)}, u32[]{:S(2)}) collective-permute-start(bf16[2560,384]{0,1:T(8,128)(2,1)S(1)} %constant_dynamic-slice_fusion.1), channel_id=1, source_target_pairs={{0,1},{1,0},{2,3},{3,2},{4,5},{5,4},{6,7},{7,6},{8,9},{9,8},{10,11... | collective-permute-start | bytes 5898248 | tf_op jit(solution)/shard_map/ppermute | solution.py:61
  20.5 66.0 %collective-permute-done = bf16[2560,384]{0,1:T(8,128)(2,1)} collective-permute-done((bf16[2560,384]{0,1:T(8,128)(2,1)S(1)}, bf16[2560,384]{0,1:T(8,128)(2,1)}, u32[]{:S(2)}, u32[]{:S(2)}) %collective-permute-start) | collective-permute-done | bytes 1966112 | tf_op jit(solution)/shard_map/ppermute | solution.py:61
  86.6 0.9 copy.27
  87.4 6.9 %all-to-all-start = ((bf16[128,8,128]{0,2,1:T(8,128)(2,1)}), bf16[128,8,128]{0,2,1:T(8,128)(2,1)S(1)}, u32[]{:S(2)}, u32[]{:S(2)}) async-start(bf16[128,8,128]{0,2,1:T(8,128)(2,1)} %bitcast.10), calls=%async_computation | async-start | bytes 524288 | tf_op jit(solution)/shard_map/all_to_all | solution.py:84
  95.8 0.6 fusion.39
  96.4 21.7 %all-gather.4.cloned.1.call-done = bf16[512,5120]{1,0:T(8,128)(2,1)} async-done(((bf16[64,5120]{1,0:T(8,128)(2,1)}), bf16[512,5120]{1,0:T(8,128)(2,1)}) %all-gather.4.cloned.1.call-update) | async-done | bytes 5242896 | tf_op jit(solution)/shard_map/all_gather | solution.py:112
  118.1 0.7 multiply_bitcast_fusion
  119.0 0.9 copy.38
  120.1 99.0 %all-gather.6.cloned.1.call-done = bf16[1,512,5120]{2,1,0:T(8,128)(2,1)} async-done(((bf16[1,128,5120]{2,1,0:T(8,128)(2,1)}), bf16[1,512,5120]{2,1,0:T(8,128)(2,1)}) %all-gather.6.cloned.1.call-update) | async-done | bytes 5242896 | tf_op jit(solution)/shard_map/all_gather | solution.py:70
  219.1 7.3 %fusion.21 = bf16[512,384]{0,1:T(8,128)(2,1)S(1)} fusion(bf16[1,512,5120]{2,1,0:T(8,128)(2,1)} %all-gather.6.cloned.1.call-done, bf16[2560,384]{0,1:T(8,128)(2,1)} %collective-permute-done.1, bf16[2560,384]{0,1:T(8,128)(2,1)} %collective-permute-done, pred[]{:T(512)S(6)} %eq.23), kind=kOutput, calls=%fused_computation.25 | convolution fusion | flops 2031157248 | bytes 9568257 | tf_op jit(solution)/shard_map/dot_general | solution.py:71
  226.4 1.5 collective-permute-start.2
  227.9 2.9 %fusion.15 = bf16[512,384]{1,0:T(8,128)(2,1)S(1)} fusion(bf16[5120,384]{0,1:T(8,128)(2,1)S(1)} %bitcast.98, bf16[1,512,5120]{2,1,0:T(8,128)(2,1)S(1)} %copy-done.6), kind=kOutput, calls=%fused_computation.23 | convolution fusion | flops 2013462528 | bytes 9568256 | tf_op jit(solution)/shard_map/dot_general | solution.py:73
  230.8 0.6 copy.23
  231.5 5.9 %collective-permute-done.2 = bf16[512,384]{0,1:T(8,128)(2,1)} collective-permute-done((bf16[512,384]{0,1:T(8,128)(2,1)S(1)}, bf16[512,384]{0,1:T(8,128)(2,1)}, u32[]{:S(2)}, u32[]{:S(2)}) %collective-permute-start.2) | collective-permute-done | bytes 393248 | tf_op jit(solution)/shard_map/ppermute | solution.py:72
  237.4 2.6 stack_reshape.10
  240.1 4.2 %broadcast_select_fusion = bf16[4,2,128,384]{2,1,0,3:T(2,128)(2,1)} fusion(pred[]{:T(512)S(6)} %eq.27, bf16[4,1,128,384]{2,1,0,3:T(2,128)(2,1)S(1)} %stack_reshape.10, bf16[4,1,128,384]{2,1,0,3:T(2,128)(2,1)S(1)} %copy.23), kind=kLoop, calls=%fused_computation.20 | loop fusion | flops 3538944 | bytes 1572865 | tf_op jit(solution)/shard_map/jit(_where)/select_n | solution.py:76
  244.2 2.4 select_n.74
  246.7 0.4 fusion.41
  247.1 0.2 fusion.26
  247.3 0.8 fusion.40
  248.1 0.5 fusion.13
  248.7 0.7 fusion.27
  249.4 0.3 fusion.24
  249.7 1.5 fusion.25
  251.3 11.2 %all_to_all.29 = bf16[8,128,128]{1,2,0:T(8,128)(2,1)S(1)} all-to-all(bf16[8,128,128]{1,2,0:T(8,128)(2,1)S(1)} %copy.37), channel_id=1, replica_groups=mesh['groups'=2,'dp'=2,'tensor'=8] {'tensor'}, dimensions={0} | all-to-all | bytes 524288 | tf_op jit(solution)/shard_map/all_to_all | solution.py:114
  262.6 0.9 fusion.42
  263.4 4.5 %fusion.1 = bf16[1,128,5120]{2,1,0:T(8,128)(2,1)} fusion(f32[128,5120]{1,0:T(8,128)S(1)} %fusion.42, bf16[128,512]{0,1:T(8,128)(2,1)S(1)} %bitcast.103, bf16[512,5120]{1,0:T(8,128)(2,1)} %collective-permute-done.3), kind=kOutput, calls=%fused_computation.2 | convolution fusion | flops 672399360 | bytes 9306112 | tf_op jit(solution)/shard_map/dot_general | solution.py:120
  (41 shorter events, 0.8 us)
Async XLA Ops:
  6.5 1.3 copy-start
  6.5 111.5 %all-gather.4.cloned.1.call-start = ((), (), s32[]{:S(2)}) async-start(), calls=%async_computation.2 | async-start | bytes 5898240 | tf_op jit(solution)/shard_map/all_gather | solution.py:112
  8.8 210.3 %all-gather.6.cloned.1.call-start = ((), (), s32[]{:S(2)}) async-start(), calls=%async_computation.3 | async-start | bytes 6553600 | tf_op jit(solution)/shard_map/all_gather | solution.py:70
  15.8 70.8 %copy-start.2 = (bf16[1,128,1024]{2,1,0:T(8,128)(2,1)S(1)}, bf16[1,128,1024]{2,1,0:T(8,128)(2,1)}, u32[]{:S(2)}) copy-start(bf16[1,128,1024]{2,1,0:T(8,128)(2,1)} %param.8) | copy-start | bytes 786436
  15.8 79.2 %copy-start.5 = (f32[8,2]{0,1:T(2,128)S(1)}, f32[8,2]{0,1:T(2,128)}, u32[]{:S(2)}) copy-start(f32[8,2]{0,1:T(2,128)} %param.11) | copy-start | bytes 196
  17.5 69.1 %collective-permute-start = (bf16[2560,384]{0,1:T(8,128)(2,1)S(1)}, bf16[2560,384]{0,1:T(8,128)(2,1)}, u32[]{:S(2)}, u32[]{:S(2)}) collective-permute-start(bf16[2560,384]{0,1:T(8,128)(2,1)S(1)} %constant_dynamic-slice_fusion.1), channel_id=1, source_target_pairs={{0,1},{1,0},{2,3},{3,2},{4,5},{5,4},{6,7},{7,6},{8,9},{9,8},{10,11... | collective-permute-start | bytes 5898248 | tf_op jit(solution)/shard_map/ppermute | solution.py:61
  86.6 33.5 %collective-permute-start.1 = (bf16[2560,384]{0,1:T(8,128)(2,1)}, bf16[2560,384]{0,1:T(8,128)(2,1)}, u32[]{:S(2)}, u32[]{:S(2)}) collective-permute-start(bf16[2560,384]{0,1:T(8,128)(2,1)} %collective-permute-done), channel_id=1, source_target_pairs={{0,8},{8,0},{1,9},{9,1},{2,10},{10,2},{3,11},{11,3},{4,12},{12,4},... | collective-permute-start | bytes 5898248 | tf_op jit(solution)/shard_map/ppermute | solution.py:62
  87.4 30.6 %all-to-all-start = ((bf16[128,8,128]{0,2,1:T(8,128)(2,1)}), bf16[128,8,128]{0,2,1:T(8,128)(2,1)S(1)}, u32[]{:S(2)}, u32[]{:S(2)}) async-start(bf16[128,8,128]{0,2,1:T(8,128)(2,1)} %bitcast.10), calls=%async_computation | async-start | bytes 524288 | tf_op jit(solution)/shard_map/all_to_all | solution.py:84
  96.4 130.0 %copy-start.4 = (s32[1024]{0:T(1024)}, s32[1024]{0:T(1024)S(1)}, u32[]{:S(2)}) copy-start(s32[1024]{0:T(1024)S(1)} %iota.19) | copy-start | bytes 12292
  118.0 145.4 %collective-permute-start.3 = (bf16[512,5120]{1,0:T(8,128)(2,1)}, bf16[512,5120]{1,0:T(8,128)(2,1)}, u32[]{:S(2)}, u32[]{:S(2)}) collective-permute-start(bf16[512,5120]{1,0:T(8,128)(2,1)} %all-gather.4.cloned.1.call-done), channel_id=1, source_target_pairs={{0,8},{8,0},{1,9},{9,1},{2,10},{10,2},{3,11},{11,3},{4,12},{12,4},... | collective-permute-start | bytes 15728648 | tf_op jit(solution)/shard_map/ppermute | solution.py:113
  219.0 8.9 %copy-start.1 = (bf16[5120,3,128]{0,2,1:T(8,128)(2,1)S(1)}, bf16[5120,3,128]{0,2,1:T(8,128)(2,1)}, u32[]{:S(2)}) copy-start(bf16[5120,3,128]{0,2,1:T(8,128)(2,1)} %copy.22) | copy-start | bytes 11796484
  219.0 8.9 %copy-start.6 = (bf16[1,512,5120]{2,1,0:T(8,128)(2,1)S(1)}, bf16[1,512,5120]{2,1,0:T(8,128)(2,1)}, u32[]{:S(2)}) copy-start(bf16[1,512,5120]{2,1,0:T(8,128)(2,1)} %all-gather.6.cloned.1.call-done) | copy-start | bytes 15728644
  226.4 11.0 %collective-permute-start.2 = (bf16[512,384]{0,1:T(8,128)(2,1)S(1)}, bf16[512,384]{0,1:T(8,128)(2,1)}, u32[]{:S(2)}, u32[]{:S(2)}) collective-permute-start(bf16[512,384]{0,1:T(8,128)(2,1)S(1)} %fusion.21), channel_id=1, source_target_pairs={{0,1},{1,0},{2,3},{3,2},{4,5},{5,4},{6,7},{7,6},{8,9},{9,8},{10,11... | collective-permute-start | bytes 1179656 | tf_op jit(solution)/shard_map/ppermute | solution.py:72
  231.5 15.2 %slice-start.2 = ((s32[1024]{0:T(1024)}), s32[512]{0:T(512)S(1)}, s32[]{:S(2)}) async-start(s32[1024]{0:T(1024)} %copy-done.4), calls=%async_computation.6 | async-start | bytes 4096 | tf_op jit(solution)/shard_map/slice | solution.py:29
  247.3 2.0 copy-start.3
  249.3 13.2 %slice-start = ((s8[5242880]{0:T(1024)(128)(4,1)}), s8[4194304]{0:T(1024)(128)(4,1)S(1)}, s32[]{:S(2)}) async-start(s8[5242880]{0:T(1024)(128)(4,1)} %bitcast.95), calls=%async_computation.4 | async-start | bytes 8388608
  249.7 12.8 %slice-start.1 = ((s8[5242880]{0:T(1024)(128)(4,1)}), s8[1048576]{0:T(1024)(128)(4,1)S(1)}, s32[]{:S(2)}) async-start(s8[5242880]{0:T(1024)(128)(4,1)} %bitcast.95), calls=%async_computation.5 | async-start | bytes 2097152
Sparse Core Ops, SparseCore 0:
  9.5 108.4 all-gather.3
  119.6 99.3 all-gather.5

commit v2 on v1

--- a/solution.py
+++ b/solution.py
@@ -1,8 +1,11 @@
+import functools
 import math
 
 import jax
 import jax.numpy as jnp
 from jax import lax
+from jax.experimental import pallas as pl
+from jax.experimental.pallas import tpu as pltpu
 from jax.sharding import PartitionSpec as P
 
 NEG_FILL = -1e30
@@ -121,6 +124,360 @@
     return out.astype(jnp.bfloat16)[None]
 
 
+PIECES = 2
+MESH = pl.DeviceIdType.MESH
+
+
+def gather_project(
+    line, rows_ref, w_ref, ow_ref, qkv_ref, wf_ref,
+    hid, own_w, pair_w, own_o, staged,
+    load_sem, hs_sem, hr_sem, ws_sem, wr_sem, os_sem, or_sem, xs_sem, xr_sem,
+    ys_sem, yr_sem, ds_sem, dr_sem, es_sem, er_sem, ps_sem, pr_sem,
+):
+    group, core, rank = lax.axis_index("groups"), lax.axis_index("dp"), lax.axis_index("tensor")
+    spot, side = rank // PAIR, rank % PAIR
+    steps = line - 1
+    own_rows, width = rows_ref.shape
+    half = width // 2
+    quarter = ow_ref.shape[0] // 4
+    mine = group * 2 + core
+    across = (1 - group) * 2 + core
+    left, right = (group, core, rank - PAIR), (group, core, rank + PAIR)
+    partner = (group, core, spot * PAIR + 1 - side)
+    opposite = (1 - group, core, rank)
+    sibling = (group, 1 - core, rank)
+    has_left, has_right = spot > 0, spot < steps
+
+    barrier = pltpu.get_barrier_semaphore()
+    for there in (partner, opposite, sibling):
+        pl.semaphore_signal(barrier, inc=1, device_id=there, device_id_type=MESH)
+
+    @pl.when(has_left)
+    def _():
+        pl.semaphore_signal(barrier, inc=1, device_id=left, device_id_type=MESH)
+
+    @pl.when(has_right)
+    def _():
+        pl.semaphore_signal(barrier, inc=1, device_id=right, device_id_type=MESH)
+
+    loads = [
+        pltpu.make_async_copy(rows_ref, hid.at[spot], load_sem.at[0]),
+        pltpu.make_async_copy(ow_ref, own_o, load_sem.at[1]),
+        pltpu.make_async_copy(w_ref, own_w, load_sem.at[2]),
+    ]
+    for load in loads:
+        load.start()
+    pl.semaphore_wait(barrier, 3 + jnp.where(has_left, 1, 0) + jnp.where(has_right, 1, 0))
+
+    def send(src, dst, s_sem, r_sem, there):
+        return pltpu.make_async_remote_copy(
+            src_ref=src, dst_ref=dst, send_sem=s_sem, recv_sem=r_sem, device_id=there, device_id_type=MESH
+        )
+
+    def wf(column, q):
+        return wf_ref.at[column, pl.ds(q * quarter, quarter), :]
+
+    def chunk(way, k):
+        return spot - 1 - k if way == 0 else spot + 1 + k
+
+    def arrives(way, k):
+        return k < spot if way == 0 else spot + 1 + k < line
+
+    def leaves(way, k):
+        if way == 0:
+            return jnp.logical_and(k <= spot, has_right)
+        return jnp.logical_and(spot + k < line, has_left)
+
+    def carried(way, k):
+        return spot - k if way == 0 else spot + k
+
+    def ahead(way):
+        return right if way == 0 else left
+
+    piece = own_rows // PIECES
+
+    def hid_copy(way, k, p, at):
+        cut = pl.ds(p * piece, piece)
+        source = rows_ref.at[cut, :] if k == 0 else hid.at[at, cut, :]
+        return send(source, hid.at[at, cut, :], hs_sem.at[way, k, p], hr_sem.at[way, k, p], ahead(way))
+
+    def out_copy(way, k, at):
+        column = at * PAIR + side
+        source = ow_ref.at[pl.ds(mine * quarter, quarter), :] if k == 0 else wf(column, mine)
+        return send(source, wf(column, mine), os_sem.at[way, k], or_sem.at[way, k], ahead(way))
+
+    def pair_copy(slot, column, source):
+        return send(source, wf(column, mine), xs_sem.at[slot], xr_sem.at[slot], partner)
+
+    def y_copy(slot, column):
+        return send(wf(column, mine), wf(column, mine), ys_sem.at[slot], yr_sem.at[slot], opposite)
+
+    def y_arrival(slot, column):
+        return send(wf(column, across), wf(column, across), ys_sem.at[slot], yr_sem.at[slot], opposite)
+
+    def d_copy(slot, column, q):
+        return send(wf(column, q), wf(column, q), ds_sem.at[slot], dr_sem.at[slot], sibling)
+
+    def e_copy(slot, column, q):
+        return send(wf(column, q), wf(column, q), es_sem.at[slot], er_sem.at[slot], sibling)
+
+    def spread(slot, column):
+        y_copy(slot, column).start()
+        d_copy(slot, column, mine).start()
+
+    last = 2 * steps
+    all_slots = [(way * steps + k, way, k) for k in range(steps) for way in (0, 1)]
+    partner_column = spot * PAIR + 1 - side
+
+    for way in (0, 1):
+
+        @pl.when(leaves(way, 0))
+        def _():
+            out_copy(way, 0, spot).start()
+            for p in range(PIECES):
+                hid_copy(way, 0, p, spot).start()
+
+    own_quarter = ow_ref.at[pl.ds(mine * quarter, quarter), :]
+    pair_copy(last, rank, own_quarter).start()
+    cut_w = pl.ds(core * half, half)
+    other_w = pl.ds((1 - core) * half, half)
+    w_out = send(w_ref.at[:, cut_w, :], pair_w.at[:, cut_w, :], ws_sem.at[0], wr_sem.at[0], partner)
+    w_out.start()
+    for load in loads:
+        load.wait()
+    keep = pltpu.make_async_copy(own_o, wf_ref.at[rank], load_sem.at[3])
+    keep.start()
+
+    def project(at, weights, store):
+        def one(j, carry):
+            total = jnp.dot(hid[at], weights[j], preferred_element_type=jnp.float32)
+            store(j, total.astype(jnp.bfloat16))
+            return carry
+
+        lax.fori_loop(0, 3, one, 0)
+
+    def project_own(at):
+        def store(j, value):
+            qkv_ref[j, at, side] = value
+
+        project(at, own_w, store)
+
+    def swap_copy(slot, at):
+        return send(
+            staged.at[slot], qkv_ref.at[:, at, side], ps_sem.at[slot], pr_sem.at[slot], partner
+        )
+
+    def swap_arrival(slot, at):
+        return send(
+            staged.at[slot], qkv_ref.at[:, at, 1 - side], ps_sem.at[slot], pr_sem.at[slot], partner
+        )
+
+    def project_pair(slot, at):
+        def store(j, value):
+            staged[slot, j] = value
+
+        project(at, pair_w, store)
+
+    project_own(spot)
+
+    for k in range(steps):
+        for way in (0, 1):
+
+            @pl.when(arrives(way, k))
+            def _():
+                at = chunk(way, k)
+                out_copy(way, k, at).wait_recv()
+                if k + 1 < steps:
+
+                    @pl.when(leaves(way, k + 1))
+                    def _():
+                        out_copy(way, k + 1, at).start()
+
+                slot = way * steps + k
+                column = at * PAIR + side
+                pair_copy(slot, column, wf(column, mine)).start()
+                spread(slot, column)
+
+        for p in range(PIECES):
+            for way in (0, 1):
+
+                @pl.when(arrives(way, k))
+                def _():
+                    at = chunk(way, k)
+                    hid_copy(way, k, p, at).wait_recv()
+                    if k + 1 < steps:
+
+                        @pl.when(leaves(way, k + 1))
+                        def _():
+                            hid_copy(way, k + 1, p, at).start()
+
+        if k == 0:
+            pair_copy(last, partner_column, wf(partner_column, mine)).wait_recv()
+            spread(2 * last, partner_column)
+            send(
+                w_ref.at[:, cut_w, :], pair_w.at[:, cut_w, :], ws_sem.at[0], wr_sem.at[0], partner
+            ).wait_recv()
+            w_side = send(
+                pair_w.at[:, cut_w, :], pair_w.at[:, cut_w, :], ws_sem.at[1], wr_sem.at[1], sibling
+            )
+            w_side.start()
+            send(
+                pair_w.at[:, other_w, :], pair_w.at[:, other_w, :], ws_sem.at[1], wr_sem.at[1], sibling
+            ).wait_recv()
+            project_pair(last, spot)
+        for way in (0, 1):
+
+            @pl.when(arrives(way, k))
+            def _():
+                at = chunk(way, k)
+                slot = way * steps + k
+                project_pair(slot, at)
+                project_own(at)
+                swap_copy(slot, at).start()
+                column = at * PAIR + 1 - side
+                pair_copy(slot, column, wf(column, mine)).wait_recv()
+                spread(last + slot, column)
+
+        if k == 0:
+            swap_copy(last, spot).start()
+
+    columns = [(2 * last, partner_column, None)]
+    for slot, way, k in all_slots:
+        columns.append((slot, chunk(way, k) * PAIR + side, (way, k)))
+        columns.append((last + slot, chunk(way, k) * PAIR + 1 - side, (way, k)))
+
+    def each(action):
+        for slot, column, when in columns:
+            if when is None:
+                action(slot, column)
+            else:
+
+                @pl.when(arrives(*when))
+                def _():
+                    action(slot, column)
+
+    def pass_on(slot, column):
+        y_arrival(slot, column).wait_recv()
+        e_copy(slot, column, across).start()
+
+    def finish(slot, column):
+        sib_mine = group * 2 + 1 - core
+        sib_across = (1 - group) * 2 + 1 - core
+        d_copy(slot, column, sib_mine).wait_recv()
+        e_copy(slot, column, sib_across).wait_recv()
+        y_copy(slot, column).wait_send()
+        d_copy(slot, column, mine).wait_send()
+        e_copy(slot, column, across).wait_send()
+
+    each(pass_on)
+    each(finish)
+    for slot, way, k in all_slots:
+
+        @pl.when(arrives(way, k))
+        def _():
+            at = chunk(way, k)
+            swap_arrival(slot, at).wait_recv()
+            swap_copy(slot, at).wait_send()
+            column = at * PAIR + side
+            pair_copy(slot, column, wf(column, mine)).wait_send()
+
+        @pl.when(leaves(way, k))
+        def _():
+            at = carried(way, k)
+            out_copy(way, k, at).wait_send()
+            for p in range(PIECES):
+                hid_copy(way, k, p, at).wait_send()
+
+    swap_arrival(last, spot).wait_recv()
+    swap_copy(last, spot).wait_send()
+    pair_copy(last, rank, own_quarter).wait_send()
+    w_out.wait_send()
+    w_side.wait_send()
+    keep.wait()
+
+
+def gathered(local_rows, w3, out_weight, ranks):
+    line = ranks // PAIR
+    steps = line - 1
+    own_rows, width = local_rows.shape
+    head_width = w3.shape[2]
+    kind = local_rows.dtype
+    dma = pltpu.SemaphoreType.DMA
+    slots, wide = 2 * steps + 1, 4 * steps + 1
+    anywhere = pl.BlockSpec(memory_space=pltpu.HBM)
+    return pl.pallas_call(
+        functools.partial(gather_project, line),
+        out_shape=(
+            jax.ShapeDtypeStruct((3, line, PAIR, own_rows, head_width), kind),
+            jax.ShapeDtypeStruct((ranks,) + out_weight.shape, kind),
+        ),
+        in_specs=[anywhere] * 3,
+        out_specs=(pl.BlockSpec(memory_space=pltpu.VMEM), anywhere),
+        scratch_shapes=[
+            pltpu.VMEM((line, own_rows, width), kind),
+            pltpu.VMEM(w3.shape, kind),
+            pltpu.VMEM(w3.shape, kind),
+            pltpu.VMEM(out_weight.shape, kind),
+            pltpu.VMEM((slots, 3, own_rows, head_width), kind),
+            dma((4,)),
+            dma((2, steps, PIECES)), dma((2, steps, PIECES)),
+            dma((2,)), dma((2,)),
+            dma((2, steps)), dma((2, steps)),
+            dma((slots,)), dma((slots,)),
+            dma((wide,)), dma((wide,)),
+            dma((wide,)), dma((wide,)),
+            dma((wide,)), dma((wide,)),
+            dma((slots,)), dma((slots,)),
+        ],
+        compiler_params=pltpu.CompilerParams(
+            collective_id=0, has_side_effects=True, vmem_limit_bytes=48 * 1024 * 1024
+        ),
+    )(local_rows, w3, out_weight)
+
+
+def mix(values, firsts, mix_table, mix_index):
+    levels = mix_table.shape[0]
+    one_hot = (mix_index[:, None] == jnp.arange(levels, dtype=jnp.int32)[None, :]).astype(
+        jnp.float32
+    )
+    weights_mix = jnp.dot(one_hot, mix_table, precision=lax.Precision.HIGHEST)
+    return (
+        weights_mix[None, :, 0:1] * values.astype(jnp.float32)
+        + weights_mix[None, :, 1:2] * firsts.astype(jnp.float32)
+    ).astype(jnp.bfloat16)
+
+
+def body_gathered(hidden_in, first_values, qkv_weight, out_weight, mix_table, mix_index, lengths):
+    local_rows = hidden_in[0]
+    own_rows = local_rows.shape[0]
+    ranks = lax.axis_size("tensor")
+    total_rows = ranks * own_rows
+    heads_here = mix_index.shape[0]
+    head_width = qkv_weight.shape[2]
+    head_size = head_width // heads_here
+    relaid = lax.all_to_all(first_values[0], "tensor", split_axis=1, concat_axis=0, tiled=True)
+    firsts = relaid.reshape(total_rows, heads_here, head_size)
+    qkv, full_out = gathered(local_rows, qkv_weight.transpose(1, 0, 2), out_weight, ranks)
+    qkv = qkv.reshape(3, total_rows, heads_here, head_size)
+    mixed_values = mix(qkv[2], firsts, mix_table, mix_index)
+    attended = attention(qkv[0], qkv[1], mixed_values, lengths[0], head_size)
+    attended = attended.reshape(total_rows, head_width)
+    kept = lax.all_to_all(attended, "tensor", split_axis=0, concat_axis=1, tiled=True)
+    weights = full_out.reshape(ranks * head_width, full_out.shape[2])
+    return jnp.dot(kept, weights, preferred_element_type=jnp.float32).astype(jnp.bfloat16)[None]
+
+
+def chosen(hidden_in, first_values, qkv_weight, out_weight, mix_table, mix_index, lengths):
+    args = (hidden_in, first_values, qkv_weight, out_weight, mix_table, mix_index, lengths)
+    ranks = lax.axis_size("tensor")
+    total_rows = ranks * hidden_in.shape[1]
+    fits = ranks * out_weight.size * 2 <= total_rows * hidden_in.shape[2] * 4
+    two = lax.axis_size("groups") == 2 and lax.axis_size("dp") == 2
+    if fits and two:
+        return body_gathered(*args)
+    return body(*args)
+
+
 def solution(mesh):
     placed = (
         P(("groups", "dp"), "tensor", None),
@@ -132,7 +489,7 @@
         P(("groups", "dp")),
     )
     return jax.shard_map(
-        body,
+        chosen,
         mesh=mesh,
         in_specs=placed,
         out_specs=P(("groups", "dp"), "tensor", None),

time: 275 us -> 164 us (0.60)
  waiting for transfers between devices: 193 us -> 0.01 us
  Pallas kernels: 0 us -> 127 us
  local copies, waits for them, and re-layouts: 18.7 us -> 4.61 us
  between operations: 15 us -> 1.44 us
  matrix products: 18.8 us -> 9 us
  starting transfers between devices: 11.5 us -> 7.28 us
  other arithmetic: 6.28 us -> 2.1 us
    pallas_call x0 -> x1, Pallas kernels: none -> 127 us  [gathered(): pl.pallas_call(functools.partial(gather_project, line), out_shape=(jax.Sh...]
    all_gather x2 -> x0, waiting for transfers between devices: 121 us -> none  [the longest x1 99 us: body(): lax.all_gather(local_rows, 'tensor', axis=0, tiled=True, axis_index_group...]
    ppermute x4 -> x0, waiting for transfers between devices: 72 us -> none  [the longest x1 66 us: body(): got = lax.ppermute(sent, 'tensor', swap_pair)]
    dot_general x5 -> x2, matrix products: 15.7 us -> 6.8 us  [the longest x1 6.69 us: body_gathered(): jnp.dot(kept, weights, preferred_element_type=jnp.float32)]
    unnamed x22 -> x11, local copies, waits for them, and re-layouts: 9.38 us -> 2.96 us
    ppermute x4 -> x0, starting transfers between devices: 4.57 us -> none  [the longest x1 3.03 us: body(): got = lax.ppermute(sent, 'tensor', swap_pair)]
    select_n x2 -> x0, other arithmetic: 4.19 us -> none  [the longest x1 4.17 us: body(): jnp.where(side == 0, jnp.stack([ours, from_pair], axis=1), jnp.stack([fro...]
    another operation x2 -> x0, local copies, waits for them, and re-layouts: 3.27 us -> none  [body(): jnp.stack([ours, from_pair], axis=1)]
  transfers between devices with their start and end apart: 7 -> 1, of which waited for: 4 -> 0; matrix products, arithmetic and copies ran while one was open for 13% -> 2% of each run, Pallas kernels for 0% -> 77%
where the time goes in v2:
time: 164 us
  Pallas kernels  127 us (77%)
  blocking collectives  12.9 us (8%)
  matrix products  9 us (5%)
  starting transfers between devices  7.28 us (4%)
  local copies, waits for them, and re-layouts  4.61 us (3%)
  other arithmetic  2.1 us (1%)
    pallas_call x1, Pallas kernels, gathered(): pl.pallas_call(functools.partial(gather_project, line), out_shape=(jax.Sh...  127 us
    all_to_all x1, blocking collectives, body_gathered(): lax.all_to_all(attended, 'tensor', split_axis=0, concat_axis=1, tiled=True)  12.9 us
    all_to_all x1, starting transfers between devices, body_gathered(): lax.all_to_all(first_values[0], 'tensor', split_axis=1, concat_axis=0, ti...  7.28 us
    dot_general x1, matrix products, body_gathered(): jnp.dot(kept, weights, preferred_element_type=jnp.float32)  6.69 us
  transfers between devices with their start and end apart: 1, of which 0 were waited for; matrix products, arithmetic and copies ran while one was open for 2% of the time, Pallas kernels for 77%

profile of v2, /device:TPU:0, one launch (start us, length us, event | category | flops | bytes accessed | tf_op | source)
XLA Modules:
  0.0 164.0 jit_solution(8076441115275846030)
XLA Ops:
  0.0 0.0 copy-start
  0.0 0.0 copy-start.1
  0.0 1.1 copy.11
  1.1 0.8 copy.8
  1.9 7.3 %all-to-all-start = ((bf16[128,8,128]{2,0,1:T(8,128)(2,1)}), bf16[128,8,128]{2,0,1:T(8,128)(2,1)S(1)}, u32[]{:S(2)}, u32[]{:S(2)}) async-start(bf16[128,8,128]{2,0,1:T(8,128)(2,1)} %copy.8), calls=%async_computation | async-start | bytes 524288 | tf_op jit(solution)/shard_map/all_to_all | solution.py:458
  9.2 0.0 copy-done.1
  9.2 0.0 copy-start.2
  9.2 1.3 copy-done.2
  10.5 126.6 %shard_map.73 = (bf16[3,4,2,128,128]{4,3,2,1,0:T(8,128)(2,1)S(1)}, bf16[8,128,5120]{2,1,0:T(8,128)(2,1)}) custom-call(bf16[128,5120]{1,0:T(8,128)(2,1)S(1)} %bitcast.57, bf16[3,5120,128]{2,1,0:T(8,128)(2,1)} %bitcast.58, bf16[128,5120]{1,0:T(8,128)(2,1)S(1)} %copy-done.2), custom_call_target="tpu_custom_call" | custom-call | tf_op jit(solution)/shard_map/pallas_call | solution.py:408
  138.5 0.0 copy-done
  138.5 0.1 fusion.12
  138.6 0.7 fusion.16
  139.3 0.4 fusion.18
  139.7 0.0 copy-start.3
  139.7 0.2 fusion.7
  139.9 0.8 fusion.17
  140.7 0.0 copy-done.3
  140.7 0.5 fusion.3
  141.2 0.0 all-to-all-done
  141.2 0.7 convert_multiply_fusion
  141.9 0.7 convert_multiply_fusion.1
  142.6 0.0 copy-start.4
  142.6 0.7 fusion.6
  143.3 0.5 copy-done.4
  143.8 0.4 fusion.5
  144.2 0.2 copy.10
  144.4 12.9 %all_to_all.29 = bf16[8,128,128]{2,1,0:T(8,128)(2,1)S(1)} all-to-all(bf16[8,128,128]{2,1,0:T(8,128)(2,1)S(1)} %bitcast.61), channel_id=1, replica_groups=mesh['groups'=2,'dp'=2,'tensor'=8] {'tensor'}, dimensions={0} | all-to-all | bytes 524288 | tf_op jit(solution)/shard_map/all_to_all | solution.py:465
  157.3 6.7 %fusion.1 = bf16[1,128,5120]{2,1,0:T(8,128)(2,1)} fusion(bf16[8,128,5120]{2,1,0:T(8,128)(2,1)} %get-tuple-element.8, bf16[8,128,128]{2,1,0:T(8,128)(2,1)S(1)} %all_to_all.29), kind=kOutput, calls=%fused_computation.2 | convolution fusion | flops 1342832640 | bytes 12058624 | tf_op jit(solution)/shard_map/dot_general | solution.py:467
  (9 shorter events, 0.1 us)
Async XLA Ops:
  0.0 138.5 %copy-start = (f32[8,2]{0,1:T(2,128)S(1)}, f32[8,2]{0,1:T(2,128)}, u32[]{:S(2)}) copy-start(f32[8,2]{0,1:T(2,128)} %param.11) | copy-start | bytes 196
  0.0 9.2 %copy-start.1 = (bf16[1,128,5120]{2,1,0:T(8,128)(2,1)S(1)}, bf16[1,128,5120]{2,1,0:T(8,128)(2,1)}, u32[]{:S(2)}) copy-start(bf16[1,128,5120]{2,1,0:T(8,128)(2,1)} %param.7) | copy-start | bytes 3932164
  1.9 139.3 %all-to-all-start = ((bf16[128,8,128]{2,0,1:T(8,128)(2,1)}), bf16[128,8,128]{2,0,1:T(8,128)(2,1)S(1)}, u32[]{:S(2)}, u32[]{:S(2)}) async-start(bf16[128,8,128]{2,0,1:T(8,128)(2,1)} %copy.8), calls=%async_computation | async-start | bytes 524288 | tf_op jit(solution)/shard_map/all_to_all | solution.py:458
  9.2 1.3 copy-start.2
  139.7 1.0 copy-start.3
  142.6 1.2 copy-start.4

commit v3 on v2

--- a/solution.py
+++ b/solution.py
@@ -129,10 +129,10 @@
 
 
 def gather_project(
-    line, rows_ref, w_ref, ow_ref, qkv_ref, wf_ref,
-    hid, own_w, pair_w, own_o, staged,
+    line, rows_ref, w_ref, ow_ref, fv_ref, qkv_ref, wf_ref, fo_ref,
+    hid, both_w, own_o, staged,
     load_sem, hs_sem, hr_sem, ws_sem, wr_sem, os_sem, or_sem, xs_sem, xr_sem,
-    ys_sem, yr_sem, ds_sem, dr_sem, es_sem, er_sem, ps_sem, pr_sem,
+    ys_sem, yr_sem, ds_sem, dr_sem, es_sem, er_sem, ps_sem, pr_sem, fs_sem, fr_sem,
 ):
     group, core, rank = lax.axis_index("groups"), lax.axis_index("dp"), lax.axis_index("tensor")
     spot, side = rank // PAIR, rank % PAIR
@@ -149,25 +149,23 @@
     has_left, has_right = spot > 0, spot < steps
 
     barrier = pltpu.get_barrier_semaphore()
-    for there in (partner, opposite, sibling):
+    ranks = line * PAIR
+    head = w_ref.shape[2]
+    peers = [(group, core, (rank + o) % ranks) for o in range(1, ranks)]
+    for there in peers + [opposite, sibling]:
         pl.semaphore_signal(barrier, inc=1, device_id=there, device_id_type=MESH)
-
-    @pl.when(has_left)
-    def _():
-        pl.semaphore_signal(barrier, inc=1, device_id=left, device_id_type=MESH)
-
-    @pl.when(has_right)
-    def _():
-        pl.semaphore_signal(barrier, inc=1, device_id=right, device_id_type=MESH)
 
     loads = [
         pltpu.make_async_copy(rows_ref, hid.at[spot], load_sem.at[0]),
         pltpu.make_async_copy(ow_ref, own_o, load_sem.at[1]),
-        pltpu.make_async_copy(w_ref, own_w, load_sem.at[2]),
+        pltpu.make_async_copy(w_ref, both_w.at[:, :, pl.ds(0, head)], load_sem.at[2]),
+        pltpu.make_async_copy(
+            fv_ref.at[:, pl.ds(pl.multiple_of(rank * head, head), head)], fo_ref.at[rank], load_sem.at[4]
+        ),
     ]
     for load in loads:
         load.start()
-    pl.semaphore_wait(barrier, 3 + jnp.where(has_left, 1, 0) + jnp.where(has_right, 1, 0))
+    pl.semaphore_wait(barrier, ranks + 1)
 
     def send(src, dst, s_sem, r_sem, there):
         return pltpu.make_async_remote_copy(
@@ -241,26 +239,31 @@
     pair_copy(last, rank, own_quarter).start()
     cut_w = pl.ds(core * half, half)
     other_w = pl.ds((1 - core) * half, half)
-    w_out = send(w_ref.at[:, cut_w, :], pair_w.at[:, cut_w, :], ws_sem.at[0], wr_sem.at[0], partner)
+    lanes = pl.ds(head, head)
+    w_out = send(w_ref.at[:, cut_w, :], both_w.at[:, cut_w, lanes], ws_sem.at[0], wr_sem.at[0], partner)
+    first_copies = [
+        send(
+            fv_ref.at[:, pl.ds(pl.multiple_of(there[2] * head, head), head)],
+            fo_ref.at[rank], fs_sem.at[o], fr_sem.at[o], there,
+        )
+        for o, there in enumerate(peers)
+    ]
     w_out.start()
+    for copy in first_copies:
+        copy.start()
     for load in loads:
         load.wait()
     keep = pltpu.make_async_copy(own_o, wf_ref.at[rank], load_sem.at[3])
     keep.start()
 
-    def project(at, weights, store):
+    def project(slot, at):
         def one(j, carry):
-            total = jnp.dot(hid[at], weights[j], preferred_element_type=jnp.float32)
-            store(j, total.astype(jnp.bfloat16))
+            total = jnp.dot(hid[at], both_w[j], preferred_element_type=jnp.float32)
+            staged[slot, j] = total[:, head:].astype(jnp.bfloat16)
+            qkv_ref[j, at, side] = total[:, :head].astype(jnp.bfloat16)
             return carry
 
         lax.fori_loop(0, 3, one, 0)
-
-    def project_own(at):
-        def store(j, value):
-            qkv_ref[j, at, side] = value
-
-        project(at, own_w, store)
 
     def swap_copy(slot, at):
         return send(
@@ -271,14 +274,6 @@
         return send(
             staged.at[slot], qkv_ref.at[:, at, 1 - side], ps_sem.at[slot], pr_sem.at[slot], partner
         )
-
-    def project_pair(slot, at):
-        def store(j, value):
-            staged[slot, j] = value
-
-        project(at, pair_w, store)
-
-    project_own(spot)
 
     for k in range(steps):
         for way in (0, 1):
@@ -315,28 +310,27 @@
             pair_copy(last, partner_column, wf(partner_column, mine)).wait_recv()
             spread(2 * last, partner_column)
             send(
-                w_ref.at[:, cut_w, :], pair_w.at[:, cut_w, :], ws_sem.at[0], wr_sem.at[0], partner
+                w_ref.at[:, cut_w, :], both_w.at[:, cut_w, lanes], ws_sem.at[0], wr_sem.at[0], partner
             ).wait_recv()
             w_side = send(
-                pair_w.at[:, cut_w, :], pair_w.at[:, cut_w, :], ws_sem.at[1], wr_sem.at[1], sibling
+                both_w.at[:, cut_w, lanes], both_w.at[:, cut_w, lanes], ws_sem.at[1], wr_sem.at[1], sibling
             )
             w_side.start()
             send(
-                pair_w.at[:, other_w, :], pair_w.at[:, other_w, :], ws_sem.at[1], wr_sem.at[1], sibling
+                both_w.at[:, other_w, lanes], both_w.at[:, other_w, lanes], ws_sem.at[1], wr_sem.at[1], sibling
             ).wait_recv()
-            project_pair(last, spot)
+            project(last, spot)
         for way in (0, 1):
 
             @pl.when(arrives(way, k))
             def _():
                 at = chunk(way, k)
                 slot = way * steps + k
-                project_pair(slot, at)
-                project_own(at)
-                swap_copy(slot, at).start()
+                project(slot, at)
                 column = at * PAIR + 1 - side
                 pair_copy(slot, column, wf(column, mine)).wait_recv()
                 spread(last + slot, column)
+                swap_copy(slot, at).start()
 
         if k == 0:
             swap_copy(last, spot).start()
@@ -394,9 +388,63 @@
     w_out.wait_send()
     w_side.wait_send()
     keep.wait()
-
-
-def gathered(local_rows, w3, out_weight, ranks):
+    for o in range(ranks - 1):
+        send(
+            fv_ref.at[:, pl.ds(0, head)], fo_ref.at[(rank + ranks - 1 - o) % ranks],
+            fs_sem.at[o], fr_sem.at[o], peers[o],
+        ).wait_recv()
+    for copy in first_copies:
+        copy.wait_send()
+
+
+def exchange(ranks, att_ref, kept_ref, load_sem, s_sem, r_sem):
+    group, core, rank = lax.axis_index("groups"), lax.axis_index("dp"), lax.axis_index("tensor")
+    rows, head = kept_ref.shape[0], att_ref.shape[1]
+    peers = [(group, core, (rank + o) % ranks) for o in range(1, ranks)]
+    barrier = pltpu.get_barrier_semaphore()
+    for there in peers:
+        pl.semaphore_signal(barrier, inc=1, device_id=there, device_id_type=MESH)
+    pl.semaphore_wait(barrier, ranks - 1)
+
+    def block(r):
+        return att_ref.at[pl.ds(pl.multiple_of(r * rows, rows), rows), :]
+
+    def column(r):
+        return kept_ref.at[:, pl.ds(pl.multiple_of(r * head, head), head)]
+
+    def copy(o, r):
+        return pltpu.make_async_remote_copy(
+            src_ref=block(peers[o][2]), dst_ref=column(r), send_sem=s_sem.at[o], recv_sem=r_sem.at[o],
+            device_id=peers[o], device_id_type=MESH,
+        )
+
+    for o in range(ranks - 1):
+        copy(o, rank).start()
+    own = pltpu.make_async_copy(block(rank), column(rank), load_sem)
+    own.start()
+    own.wait()
+    for o in range(ranks - 1):
+        copy(o, (rank + ranks - 1 - o) % ranks).wait_recv()
+    for o in range(ranks - 1):
+        copy(o, rank).wait_send()
+
+
+def to_positions(attended, ranks):
+    total_rows, head_width = attended.shape
+    dma = pltpu.SemaphoreType.DMA
+    return pl.pallas_call(
+        functools.partial(exchange, ranks),
+        out_shape=jax.ShapeDtypeStruct((total_rows // ranks, ranks * head_width), attended.dtype),
+        in_specs=[pl.BlockSpec(memory_space=pltpu.VMEM)],
+        out_specs=pl.BlockSpec(memory_space=pltpu.VMEM),
+        scratch_shapes=[dma, dma((ranks - 1,)), dma((ranks - 1,))],
+        compiler_params=pltpu.CompilerParams(
+            collective_id=1, has_side_effects=True, vmem_limit_bytes=8 * 1024 * 1024
+        ),
+    )(attended)
+
+
+def gathered(local_rows, w3, out_weight, firsts, ranks):
     line = ranks // PAIR
     steps = line - 1
     own_rows, width = local_rows.shape
@@ -410,16 +458,20 @@
         out_shape=(
             jax.ShapeDtypeStruct((3, line, PAIR, own_rows, head_width), kind),
             jax.ShapeDtypeStruct((ranks,) + out_weight.shape, kind),
+            jax.ShapeDtypeStruct((ranks, own_rows, head_width), kind),
         ),
-        in_specs=[anywhere] * 3,
-        out_specs=(pl.BlockSpec(memory_space=pltpu.VMEM), anywhere),
+        in_specs=[anywhere] * 4,
+        out_specs=(
+            pl.BlockSpec(memory_space=pltpu.VMEM),
+            anywhere,
+            pl.BlockSpec(memory_space=pltpu.VMEM),
+        ),
         scratch_shapes=[
             pltpu.VMEM((line, own_rows, width), kind),
-            pltpu.VMEM(w3.shape, kind),
-            pltpu.VMEM(w3.shape, kind),
+            pltpu.VMEM(w3.shape[:2] + (2 * head_width,), kind),
             pltpu.VMEM(out_weight.shape, kind),
             pltpu.VMEM((slots, 3, own_rows, head_width), kind),
-            dma((4,)),
+            dma((5,)),
             dma((2, steps, PIECES)), dma((2, steps, PIECES)),
             dma((2,)), dma((2,)),
             dma((2, steps)), dma((2, steps)),
@@ -428,11 +480,12 @@
             dma((wide,)), dma((wide,)),
             dma((wide,)), dma((wide,)),
             dma((slots,)), dma((slots,)),
+            dma((ranks - 1,)), dma((ranks - 1,)),
         ],
         compiler_params=pltpu.CompilerParams(
             collective_id=0, has_side_effects=True, vmem_limit_bytes=48 * 1024 * 1024
         ),
-    )(local_rows, w3, out_weight)
+    )(local_rows, w3, out_weight, firsts)
 
 
 def mix(values, firsts, mix_table, mix_index):
@@ -455,14 +508,15 @@
     heads_here = mix_index.shape[0]
     head_width = qkv_weight.shape[2]
     head_size = head_width // heads_here
-    relaid = lax.all_to_all(first_values[0], "tensor", split_axis=1, concat_axis=0, tiled=True)
+    qkv, full_out, relaid = gathered(
+        local_rows, qkv_weight.transpose(1, 0, 2), out_weight, first_values[0], ranks
+    )
     firsts = relaid.reshape(total_rows, heads_here, head_size)
-    qkv, full_out = gathered(local_rows, qkv_weight.transpose(1, 0, 2), out_weight, ranks)
     qkv = qkv.reshape(3, total_rows, heads_here, head_size)
     mixed_values = mix(qkv[2], firsts, mix_table, mix_index)
     attended = attention(qkv[0], qkv[1], mixed_values, lengths[0], head_size)
     attended = attended.reshape(total_rows, head_width)
-    kept = lax.all_to_all(attended, "tensor", split_axis=0, concat_axis=1, tiled=True)
+    kept = to_positions(attended, ranks)
     weights = full_out.reshape(ranks * head_width, full_out.shape[2])
     return jnp.dot(kept, weights, preferred_element_type=jnp.float32).astype(jnp.bfloat16)[None]
 

time: 164 us -> 152 us (0.927)
  blocking collectives: 12.9 us -> 0 us
  Pallas kernels: 127 us -> 139 us
  starting transfers between devices: 7.28 us -> 0 us
  matrix products: 9 us -> 4.81 us
    all_to_all x1 -> x0, blocking collectives: 12.9 us -> none  [body_gathered(): lax.all_to_all(attended, 'tensor', split_axis=0, concat_axis=1, tiled=True)]
    pallas_call x0 -> x1, Pallas kernels: none -> 8.84 us  [to_positions(): pl.pallas_call(functools.partial(exchange, ranks), out_shape=jax.ShapeDty...]
    all_to_all x1 -> x0, starting transfers between devices: 7.28 us -> none  [body_gathered(): lax.all_to_all(first_values[0], 'tensor', split_axis=1, concat_axis=0, ti...]
    dot_general x1, matrix products: 6.69 us -> 2.6 us  [body_gathered(): jnp.dot(kept, weights, preferred_element_type=jnp.float32)]
    pallas_call x1, Pallas kernels: 127 us -> 130 us  [gathered(): pl.pallas_call(functools.partial(gather_project, line), out_shape=(jax.Sh...]
    unnamed x11 -> x16, local copies, waits for them, and re-layouts: 2.96 us -> 3.6 us
  transfers between devices with their start and end apart: 1 -> 0, of which waited for: 0 -> 0; matrix products, arithmetic and copies ran while one was open for 2% -> 0% of each run, Pallas kernels for 77% -> 0%
where the time goes in v3:
time: 152 us; the launch traced here: 151 us
  Pallas kernels  139 us (91%)
  matrix products  4.81 us (3%)
  local copies, waits for them, and re-layouts  4.27 us (3%)
  other arithmetic  2.17 us (1%)
    pallas_call x1, Pallas kernels, gathered(): pl.pallas_call(functools.partial(gather_project, line), out_shape=(jax.Sh...  130 us
    pallas_call x1, Pallas kernels, to_positions(): pl.pallas_call(functools.partial(exchange, ranks), out_shape=jax.ShapeDty...  8.84 us
    unnamed x16, local copies, waits for them, and re-layouts  3.6 us

profile of v3, /device:TPU:0, one launch (start us, length us, event | category | flops | bytes accessed | tf_op | source)
XLA Modules:
  0.0 151.5 jit_solution(14369910079886869476)
XLA Ops:
  0.0 0.0 copy-start
  1.3 0.0 copy-done
  1.3 0.1 fusion.10
  1.4 0.6 fusion.14
  2.1 0.0 copy-start.4
  2.1 0.0 copy-start.1
  2.1 1.3 copy-done.1
  3.4 0.0 copy-start.2
  3.4 1.3 copy-done.2
  4.7 0.0 copy-start.3
  4.7 0.9 copy-done.3
  5.7 129.9 %shard_map.73 = (bf16[3,4,2,128,128]{4,3,2,1,0:T(8,128)(2,1)S(1)}, bf16[8,128,5120]{2,1,0:T(8,128)(2,1)}, bf16[8,128,128]{2,1,0:T(8,128)(2,1)S(1)}) custom-call(bf16[128,5120]{1,0:T(8,128)(2,1)S(1)} %bitcast.46, bf16[3,5120,128]{2,1,0:T(8,128)(2,1)} %bitcast.51, bf16[128,5120]{1,0:T(8,128)(2,1)S(1)} %copy-done.2, bf16[128,1024]{1,0:T(8,128)(2,1)S(1)} %bitcast.47), custom_call_target="tpu_custom_call" | custom-call | tf_op jit(solution)/shard_map/pallas_call | solution.py:456
  135.6 0.0 copy-done.4
  135.6 0.0 slice-start.3
  135.6 0.7 convert_multiply_fusion
  136.3 0.8 convert_multiply_fusion.1
  137.1 0.0 slice-done.3
  137.1 0.4 fusion.16
  137.5 0.2 fusion.6
  137.7 0.0 slice-start
  137.7 0.4 fusion.4
  138.1 0.0 slice-start.1
  138.1 0.8 fusion.15
  138.9 0.5 fusion.2
  139.4 0.0 slice-start.2
  139.4 0.5 fusion.5
  140.0 8.8 %shard_map.74 = bf16[128,1024]{1,0:T(8,128)(2,1)S(1)} custom-call(bf16[1024,128]{1,0:T(8,128)(2,1)S(1)} %maximum_bitcast_fusion.att_ref), custom_call_target="tpu_custom_call" | custom-call | tf_op jit(solution)/shard_map/pallas_call | solution.py:435
  148.8 0.0 slice-done
  148.8 0.0 slice-done.1
  148.9 0.0 slice-done.2
  148.9 2.6 %fusion = bf16[1,128,5120]{2,1,0:T(8,128)(2,1)} fusion(bf16[128,1024]{1,0:T(8,128)(2,1)S(1)} %shard_map.74, bf16[1024,5120]{1,0:T(8,128)(2,1)S(1)} %bitcast.50), kind=kOutput, calls=%fused_computation.1 | convolution fusion | flops 1342832640 | bytes 12058624 | tf_op jit(solution)/shard_map/dot_general | solution.py:521
  (9 shorter events, 0.1 us)
Async XLA Ops:
  0.0 1.3 copy-start
  2.1 133.5 %copy-start.4 = (s32[1024]{0:T(1024)}, s32[1024]{0:T(1024)S(1)}, u32[]{:S(2)}) copy-start(s32[1024]{0:T(1024)S(1)} %iota.19) | copy-start | bytes 12292
  2.1 1.3 copy-start.1
  3.4 1.3 copy-start.2
  4.7 0.9 copy-start.3
  135.6 1.5 slice-start.3
  137.7 11.1 %slice-start = ((s8[10485760]{0:T(1024)(128)(4,1)}), s8[4194304]{0:T(1024)(128)(4,1)S(1)}, s32[]{:S(2)}) async-start(s8[10485760]{0:T(1024)(128)(4,1)} %bitcast.48), calls=%async_computation | async-start | bytes 8388608
  138.1 10.7 %slice-start.1 = ((s8[10485760]{0:T(1024)(128)(4,1)}), s8[4194304]{0:T(1024)(128)(4,1)S(1)}, s32[]{:S(2)}) async-start(s8[10485760]{0:T(1024)(128)(4,1)} %bitcast.48), calls=%async_computation.1 | async-start | bytes 8388608
  139.4 9.4 %slice-start.2 = ((s8[10485760]{0:T(1024)(128)(4,1)}), s8[2097152]{0:T(1024)(128)(4,1)S(1)}, s32[]{:S(2)}) async-start(s8[10485760]{0:T(1024)(128)(4,1)} %bitcast.48), calls=%async_computation.2 | async-start | bytes 4194304
